TPU v7x, 256 devices: a whole 4x4x8 slice. The times are simulated.
256 devices in a mesh: freq: 4 (over x_hi, core), rcv: 64 (over y, z, x_lo).
Axes of the slice: x: 4 (x_hi: 2, x_lo: 2; x = x_hi * 2 + x_lo), y: 4, z: 8, core: 2. Of those that a mesh axis runs over, the one named last changes fastest.
Arguments:
- reflection: bfloat16 [8, 2, 2560, 2560], P('freq', None, 'rcv'), may hold values from -5 to 5, as said below
- starts: int32 [2560, 192], P('rcv'), may hold values from 8 to 56
- focusing: float32 [8, 2560, 2, 192], P('freq', 'rcv'), may hold values from -6 to 6
- residual: float32 [8, 2560, 2, 192], P('freq', 'rcv'), may hold values from -6 to 6
- direction: float32 [8, 2560, 2, 192], P('freq', 'rcv'), may hold values from -6 to 6
- gradient: float32 [8, 2560, 2, 192], P('freq', 'rcv'), may hold values from -30 to 30
Outputs:
- new_focusing: float32 [8, 2560, 2, 192], P('freq', 'rcv')
- new_residual: float32 [8, 2560, 2, 192], P('freq', 'rcv')
- new_direction: float32 [8, 2560, 2, 192], P('freq', 'rcv')
- green_field: float32 [8, 2560, 2, 192], P('freq', 'rcv')
- focal_correlation: float32 [8, 2, 192], P('freq')
Inputs may be any that keep to these rules, and one draw needn't show every extreme that they name: Each frequency's matrix is symmetric in source and receiver: reflection[f, c, s, r] = reflection[f, c, r, s].
All inputs are finite; a program needn't handle non-finite values.
Results may differ from a plain program's by a relative error of at most 0.0003.
The roundings to bfloat16 on the way count: a program that leaves them out, or rounds other values in their place, can miss the bound.
Values may be sent and summed in bfloat16 or wider, within the bound.
A program may use at most 64 MiB of HBM per device.

v0:
```python
import math
import jax
import jax.numpy as jnp
from jax import lax
from jax.sharding import Mesh
from jax.sharding import PartitionSpec as P

N = 2560
F = 8
TS = 64
FREQ = ("freq_0", "freq_1")
RCV = ("rcv_0", "rcv_1", "rcv_2")
FREQ_RCV = ("freq_0", "freq_1", "rcv_0", "rcv_1", "rcv_2")
band_start = 5
tiny = 1e-06
highest = lax.Precision.HIGHEST


def in_order(pieces, dim):
    lengths = list(pieces.shape[1:])
    lengths[dim] *= pieces.shape[0]
    return jnp.moveaxis(pieces, 0, dim).reshape(lengths)


def sent_to_all(value, axis):
    count = lax.axis_size(axis)
    return lax.all_to_all(
        jnp.broadcast_to(value[None], (count, *value.shape)), axis, 0, 0, tiled=True
    )


def gather_directly(value, axis, dim):
    return in_order(sent_to_all(value, axis), dim)


def one_axis_at_a_time(value, axes):
    for axis in axes:
        value = lax.psum(value, axis)
    return value


def all_blocks(value, axes, sequence):
    pieces = value
    for k in sequence:
        pieces = lax.all_gather(pieces, axes[k])
    done = sequence[::-1]
    back = [done.index(k) for k in range(len(axes))]
    pieces = pieces.transpose(*back, *range(len(axes), pieces.ndim))
    return pieces.reshape(-1, *value.shape)


def gathered_by_axis(value, axes, sequence, dim):
    return in_order(all_blocks(value, axes, sequence), dim)


def of_everyone(value, axis):
    everything = sent_to_all(value, axis)
    return jnp.sum(everything, axis=0)


def tables(count, offset):
    times = jnp.arange(TS, dtype=jnp.float32)[:, None]
    bins = (jnp.arange(count, dtype=jnp.int32) + offset + band_start).astype(jnp.float32)[None, :]
    phase = 2.0 * jnp.pi * times * bins / TS
    return (jnp.cos(phase), jnp.sin(phase))


def contract_time(table, values):
    return jnp.einsum("tf,frk->trk", table, values, precision=highest)


def contract_back(table, values):
    return jnp.einsum("tf,trk->frk", table, values, precision=highest)


def time_gate(field, forward_cos, forward_sin, back_cos, back_sin, limits, complement):
    real_part = field[:, :, 0]
    imag_part = field[:, :, 1]
    time_real = contract_time(forward_cos, real_part) - contract_time(forward_sin, imag_part)
    time_imag = contract_time(forward_sin, real_part) + contract_time(forward_cos, imag_part)
    clock = jnp.arange(TS, dtype=jnp.int32)[:, None, None]
    window = (clock < limits[None]).astype(jnp.float32)
    if complement:
        window = 1.0 - window
    kept_real = window * time_real
    kept_imag = window * time_imag
    out_real = (contract_back(back_cos, kept_real) + contract_back(back_sin, kept_imag)) / TS
    out_imag = (contract_back(back_cos, kept_imag) - contract_back(back_sin, kept_real)) / TS
    return jnp.stack([out_real, out_imag], axis=2)


def combine(total, conjugate):
    if conjugate:
        out_real = total[:, 0, :, 0] + total[:, 1, :, 1]
        out_imag = total[:, 0, :, 1] - total[:, 1, :, 0]
    else:
        out_real = total[:, 0, :, 0] - total[:, 1, :, 1]
        out_imag = total[:, 0, :, 1] + total[:, 1, :, 0]
    return jnp.stack([out_real, out_imag], axis=2)


def per_device(reflection, starts, focusing, residual, direction, gradient):
    local_freq = reflection.shape[0]
    position = lax.axis_index(FREQ)
    cos_table, sin_table = tables(F, 0)
    own_cos, own_sin = tables(local_freq, position * local_freq)

    def gate(field, complement):
        whole = gather_directly(field, FREQ, 0)
        return time_gate(whole, cos_table, sin_table, own_cos, own_sin, starts, complement)

    def accumulate(piece):
        return jnp.einsum("fpnm,fmqk->fpnqk", reflection, piece, preferred_element_type=jnp.float32)

    direction_low = direction.astype(jnp.bfloat16)
    focusing_low = focusing.astype(jnp.bfloat16)
    aimed_total = accumulate(lax.all_gather(direction_low, RCV, axis=1, tiled=True))
    direction_image = combine(aimed_total, False)
    image = gate(direction_image, False)
    gamma, curvature = (
        one_axis_at_a_time(jnp.sum(gradient * gradient), FREQ_RCV),
        one_axis_at_a_time(jnp.sum(image * image), FREQ_RCV),
    )
    alpha = gamma / (curvature + tiny)
    new_focusing = focusing + alpha * direction
    new_residual = residual - alpha * image
    gated = gate(new_residual, False).astype(jnp.bfloat16)
    total = accumulate(gathered_by_axis(gated, RCV, (2, 0, 1), 1))
    new_gradient = combine(total, True)
    new_gamma = one_axis_at_a_time(jnp.sum(new_gradient * new_gradient), FREQ_RCV)
    new_direction = new_gradient + new_gamma / (gamma + tiny) * direction
    focus_total = accumulate(lax.all_gather(focusing_low, RCV, axis=1, tiled=True))
    focusing_image = combine(focus_total, False)
    green_field = gate(focusing_image + alpha * direction_image, True)
    corr_real = jnp.sum(
        green_field[:, :, 0] * new_focusing[:, :, 0] + green_field[:, :, 1] * new_focusing[:, :, 1],
        axis=1,
    )
    corr_imag = jnp.sum(
        green_field[:, :, 1] * new_focusing[:, :, 0] - green_field[:, :, 0] * new_focusing[:, :, 1],
        axis=1,
    )
    partial_corr = jnp.stack([corr_real, corr_imag], axis=1)
    focal_correlation = of_everyone(partial_corr, RCV) / math.sqrt(N)
    return (new_focusing, new_residual, new_direction, green_field, focal_correlation)


def solution(mesh):
    finer = Mesh(
        mesh.devices.reshape(2, 2, 4, 8, 2), ("freq_0", "freq_1", "rcv_0", "rcv_1", "rcv_2")
    )
    in_specs = (
        P(FREQ, None, RCV, None),
        P(RCV, None),
        P(FREQ, RCV, None, None),
        P(FREQ, RCV, None, None),
        P(FREQ, RCV, None, None),
        P(FREQ, RCV, None, None),
    )
    out_specs = (
        P(FREQ, RCV, None, None),
        P(FREQ, RCV, None, None),
        P(FREQ, RCV, None, None),
        P(FREQ, RCV, None, None),
        P(FREQ, None, None),
    )
    return jax.shard_map(
        per_device, mesh=finer, in_specs=in_specs, out_specs=out_specs, check_vma=False
    )
```

profile of v0, /device:TPU:4, one launch (start us, length us, event | category | flops | bytes accessed | tf_op | source)
XLA Modules:
  0.0 782.8 jit_solution(11673476122548457123)
XLA Ops:
  7.2 1.6 copy.290
  8.9 1.6 copy.289
  10.5 307.9 %all-gather.6.cloned.1.call-done = bf16[2,2560,2,192]{3,1,2,0:T(8,128)(2,1)} async-done(((bf16[2,40,2,192]{3,1,2,0:T(8,128)(2,1)}), bf16[2,2560,2,192]{3,1,2,0:T(8,128)(2,1)}) %all-gather.6.cloned.1.call-update) | async-done | bytes 3932176 | tf_op jit(solution)/shard_map/all_gather | solution.py:117
  318.5 3.5 fusion
  323.2 4.8 all-to-all-start
  328.8 12.3 %all-to-all-done = f32[4,2,40,2,192]{4,1,2,3,0:T(2,128)S(1)} async-done(((f32[4,2,40,2,192]{4,1,2,3,0:T(2,128)}), f32[4,2,40,2,192]{4,1,2,3,0:T(2,128)S(1)}, u32[]{:S(2)}, u32[]{:S(2)}) %all-to-all-start) | async-done | bytes 491552 | tf_op jit(solution)/shard_map/all_to_all | solution.py:27
  341.8 2.4 fusion.7
  344.1 2.5 add_select_fusion.1
  346.7 1.4 fusion.115
  349.5 2.4 fusion.8
  351.8 2.5 subtract_select_fusion.1
  354.4 1.6 fusion.103
  358.0 7.1 all-reduce.4
  365.1 3.1 all-reduce.3
  368.1 8.3 %all-reduce.1 = (f32[]{:T(128)}, f32[]{:T(128)}) all-reduce(f32[]{:T(128)} %get-tuple-element.38, f32[]{:T(128)} %get-tuple-element.39), channel_id=1, replica_groups=mesh['freq_0'=2,'freq_1'=2,'rcv_0'=4,'rcv_1'=8,'rcv_2'=2] {'rcv_0'}, use_global_device_ids=true, to_apply=%region_3.0 | all-reduce | flops 2 | bytes 16 | tf_op jit(solution)/shard_map/psum | solution.py:38
  376.5 20.8 %all-reduce = (f32[]{:T(128)}, f32[]{:T(128)}) all-reduce(f32[]{:T(128)} %get-tuple-element.34, f32[]{:T(128)} %get-tuple-element.35), channel_id=1, replica_groups=mesh['freq_0'=2,'freq_1'=2,'rcv_0'=4,'rcv_1'=8,'rcv_2'=2] {'rcv_1'}, use_global_device_ids=true, to_apply=%region_4.0 | all-reduce | flops 2 | bytes 16 | tf_op jit(solution)/shard_map/psum | solution.py:38
  397.3 5.8 all-reduce.2
  405.4 18.5 %all_to_all.20 = f32[4,2,40,2,192]{4,1,2,3,0:T(2,128)S(1)} all-to-all(f32[4,2,40,2,192]{4,1,2,3,0:T(2,128)S(1)} %broadcast_in_dim.9), channel_id=1, replica_groups=mesh['freq_0'=2,'freq_1'=2,'rcv_0'=4,'rcv_1'=8,'rcv_2'=2] {'freq_0','fre..., dimensions={0} | all-to-all | bytes 983040 | tf_op jit(solution)/shard_map/all_to_all | solution.py:27
  424.6 2.4 fusion.10
  427.0 2.5 subtract_select_fusion
  429.5 1.4 fusion.99
  430.9 2.4 fusion.9
  433.3 2.5 add_select_fusion
  437.2 1.8 fusion.101
  440.4 6.1 all_gather.23
  446.6 15.6 %all-gather = bf16[8,2,40,2,192]{4,2,3,1,0:T(8,128)(2,1)} all-gather(bf16[2,2,40,2,192]{4,2,3,1,0:T(8,128)(2,1)S(1)} %all_gather.23), channel_id=2, replica_groups=mesh['freq_0'=2,'freq_1'=2,'rcv_0'=4,'rcv_1'=8,'rcv_2'=2] {'rcv_0'}, dimensions={0}, use_global_device_ids=true | all-gather | bytes 614400 | tf_op jit(solution)/shard_map/all_gather | solution.py:45
  462.2 162.9 %all-gather.8.cloned.1.call-done = bf16[2,2560,2,192]{3,1,2,0:T(8,128)(2,1)} async-done(((bf16[2,40,2,192]{3,1,2,0:T(8,128)(2,1)}), bf16[2,2560,2,192]{3,1,2,0:T(8,128)(2,1)}) %all-gather.8.cloned.1.call-update) | async-done | bytes 3932176 | tf_op jit(solution)/shard_map/all_gather | solution.py:132
  625.1 3.5 fusion.2
  629.8 4.8 all-to-all-start.2
  635.3 7.9 %all-to-all-done.2 = f32[4,2,40,2,192]{4,1,2,3,0:T(2,128)S(1)} async-done(((f32[4,2,40,2,192]{4,1,2,3,0:T(2,128)}), f32[4,2,40,2,192]{4,1,2,3,0:T(2,128)S(1)}, u32[]{:S(2)}, u32[]{:S(2)}) %all-to-all-start.2) | async-done | bytes 491552 | tf_op jit(solution)/shard_map/all_to_all | solution.py:27
  643.9 2.4 fusion.11
  646.3 3.9 fusion.12
  650.1 3.7 add_multiply_fusion
  653.8 34.5 %all-gather.10.cloned.1.call-done = bf16[32,2,2,40,2,192]{5,3,4,2,1,0:T(8,128)(2,1)} async-done(((bf16[4,2,2,40,2,192]{5,3,4,2,1,0:T(8,128)(2,1)}), bf16[32,2,2,40,2,192]{5,3,4,2,1,0:T(8,128)(2,1)}) %all-gather.10.cloned.1.call-update) | async-done | bytes 3932176 | tf_op jit(solution)/shard_map/all_gather | solution.py:45
  688.3 3.0 copy.180
  694.3 4.3 subtract_multiply_fusion
  698.6 7.1 psum.115
  705.7 3.8 fusion.109
  709.4 3.3 psum.116
  712.7 3.7 fusion.95
  716.4 11.1 %psum.117 = f32[]{:T(128)} all-reduce(f32[]{:T(128)} %psum.116), channel_id=1, replica_groups=mesh['freq_0'=2,'freq_1'=2,'rcv_0'=4,'rcv_1'=8,'rcv_2'=2] {'rcv_0'}, use_global_device_ids=true, to_apply=%region_15.0 | all-reduce | flops 1 | bytes 8 | tf_op jit(solution)/shard_map/psum | solution.py:38
  727.5 2.0 fusion.97
  729.5 16.1 %psum.118 = f32[]{:T(128)} all-reduce(f32[]{:T(128)} %psum.117), channel_id=1, replica_groups=mesh['freq_0'=2,'freq_1'=2,'rcv_0'=4,'rcv_1'=8,'rcv_2'=2] {'rcv_1'}, use_global_device_ids=true, to_apply=%region_16.0 | all-reduce | flops 1 | bytes 8 | tf_op jit(solution)/shard_map/psum | solution.py:38
  745.7 2.0 fusion.107
  747.7 5.5 psum.119
  756.9 7.5 all-to-all-start.3
  764.3 1.7 copy.198
  768.4 6.9 all-to-all-done.3
  (74 shorter events, 21.5 us)
Async XLA Ops:
  7.2 311.3 %copy-start = (bf16[2,2,40,2560]{3,2,1,0:T(8,128)(2,1)S(1)}, bf16[2,2,40,2560]{3,2,1,0:T(8,128)(2,1)}, u32[]{:S(2)}) copy-start(bf16[2,2,40,2560]{3,2,1,0:T(8,128)(2,1)} %param.6) | copy-start | bytes 2457604
  7.2 311.3 %all-gather.6.cloned.1.call-start = ((), (), s32[]{:S(2)}) async-start(), calls=%async_computation.4 | async-start | bytes 5324800 | tf_op jit(solution)/shard_map/all_gather | solution.py:117
  8.9 616.2 %all-gather.8.cloned.1.call-start = ((), (), s32[]{:S(2)}) async-start(), calls=%async_computation.5 | async-start | bytes 5324800 | tf_op jit(solution)/shard_map/all_gather | solution.py:132
  322.0 6.0 copy-start.8
  323.2 17.9 %all-to-all-start = ((f32[4,2,40,2,192]{4,1,2,3,0:T(2,128)}), f32[4,2,40,2,192]{4,1,2,3,0:T(2,128)S(1)}, u32[]{:S(2)}, u32[]{:S(2)}) async-start(f32[4,2,40,2,192]{4,1,2,3,0:T(2,128)} %broadcast_in_dim.8), calls=%async_computation | async-start | bytes 1310720 | tf_op jit(solution)/shard_map/all_to_all | solution.py:27
  328.0 360.4 %all-gather.10.cloned.1.call-start = ((), (), s32[]{:S(2)}) async-start(), calls=%async_computation.6 | async-start | bytes 5898240 | tf_op jit(solution)/shard_map/all_gather | solution.py:45
  328.8 15.4 %copy-start.4 = (s32[40,192]{1,0:T(8,128)S(1)}, s32[40,192]{1,0:T(8,128)}, u32[]{:S(2)}) copy-start(s32[40,192]{1,0:T(8,128)} %param.7) | copy-start | bytes 92164
  354.4 50.0 %copy-start.9 = (f32[2,40,2,192]{3,2,1,0:T(2,128)S(1)}, f32[2,40,2,192]{3,2,1,0:T(2,128)}, u32[]{:S(2)}) copy-start(f32[2,40,2,192]{3,2,1,0:T(2,128)} %param.9) | copy-start | bytes 368644
  404.4 0.7 copy-start.5
  629.8 13.4 %all-to-all-start.2 = ((f32[4,2,40,2,192]{4,1,2,3,0:T(2,128)}), f32[4,2,40,2,192]{4,1,2,3,0:T(2,128)S(1)}, u32[]{:S(2)}, u32[]{:S(2)}) async-start(f32[4,2,40,2,192]{4,1,2,3,0:T(2,128)} %broadcast_in_dim.10), calls=%async_computation.2 | async-start | bytes 1310720 | tf_op jit(solution)/shard_map/all_to_all | solution.py:27
  643.9 2.4 copy-start.2
  691.4 3.0 copy-start.1
  691.4 3.0 copy-start.3
  692.4 0.6 copy-start.6
  693.1 0.6 copy-start.7
  756.9 18.5 %all-to-all-start.3 = ((f32[64,2,2,192]{3,2,1,0:T(2,128)}), f32[64,2,2,192]{3,2,1,0:T(2,128)S(1)}, u32[]{:S(2)}, u32[]{:S(2)}) async-start(f32[64,2,2,192]{3,2,1,0:T(2,128)} %broadcast_in_dim.11), calls=%async_computation.3 | async-start | bytes 524288 | tf_op jit(solution)/shard_map/all_to_all | solution.py:27
Sparse Core Ops, SparseCore 0:
  10.4 308.0 all-gather.5
  320.8 304.2 all-gather.7
  626.9 61.3 all-gather.9
where the time goes:
time: 793 us; the launch traced here: 783 us
  waiting for transfers between devices  533 us (67%)
  blocking collectives  128 us (16%)
  matrix products  65.1 us (8%)
  local copies, waits for them, and re-layouts  17.5 us (2%)
  starting transfers between devices  17.1 us (2%)
  between operations  16.9 us (2%)
    all_gather x1, waiting for transfers between devices, per_device(): lax.all_gather(direction_low, RCV, axis=1, tiled=True)  308 us
    all_gather x1, waiting for transfers between devices, per_device(): lax.all_gather(focusing_low, RCV, axis=1, tiled=True)  163 us
    psum x10, blocking collectives, one_axis_at_a_time(): value = lax.psum(value, axis)  88.1 us
    all_gather x1, waiting for transfers between devices, all_blocks(): pieces = lax.all_gather(pieces, axes[k])  34.5 us
    dot_general x12, matrix products, contract_time(): return jnp.einsum('tf,frk->trk', table, values, precision=highest)  33.8 us
    all_to_all x3, waiting for transfers between devices, sent_to_all(): lax.all_to_all(jnp.broadcast_to(value[None], (count, *value.shape)), axis...  27.2 us
    dot_general x12, matrix products, contract_back(): return jnp.einsum('tf,trk->frk', table, values, precision=highest)  23.2 us
    all_gather x2, blocking collectives, all_blocks(): pieces = lax.all_gather(pieces, axes[k])  21.7 us
  transfers between devices with their start and end apart: 6, of which 6 were waited for; matrix products, arithmetic and copies ran while one was open for 8% of the time, Pallas kernels for 0%

commit v1 on v0

--- a/solution.py
+++ b/solution.py
@@ -114,7 +114,11 @@
 
     direction_low = direction.astype(jnp.bfloat16)
     focusing_low = focusing.astype(jnp.bfloat16)
-    aimed_total = accumulate(lax.all_gather(direction_low, RCV, axis=1, tiled=True))
+    aimed_total = accumulate(
+        jnp.concatenate(
+            lax.all_to_all(jnp.stack([direction_low] * lax.axis_size(RCV)), RCV, 0, 0), axis=1
+        )
+    )
     direction_image = combine(aimed_total, False)
     image = gate(direction_image, False)
     gamma, curvature = (

time: 793 us -> 514 us (0.65)
  waiting for transfers between devices: 533 us -> 248 us
  starting transfers between devices: 17.1 us -> 30.8 us
    all_gather x1 -> x0, waiting for transfers between devices: 308 us -> none  [per_device(): lax.all_gather(direction_low, RCV, axis=1, tiled=True)]
    all_to_all x0 -> x1, waiting for transfers between devices: none -> 141 us  [per_device(): lax.all_to_all(jnp.stack([direction_low] * lax.axis_size(RCV)), RCV, 0, 0)]
    all_gather x1, waiting for transfers between devices: 163 us -> 47.2 us  [per_device(): lax.all_gather(focusing_low, RCV, axis=1, tiled=True)]
    all_to_all x0 -> x1, starting transfers between devices: none -> 13.1 us  [per_device(): lax.all_to_all(jnp.stack([direction_low] * lax.axis_size(RCV)), RCV, 0, 0)]
  transfers between devices with their start and end apart: 6 -> 6, of which waited for: 6 -> 6; matrix products, arithmetic and copies ran while one was open for 8% -> 12% of each run, Pallas kernels for 0% -> 0%
where the time goes in v1:
time: 514 us; the launch traced here: 510 us
  waiting for transfers between devices  248 us (48%)
  blocking collectives  124 us (24%)
  matrix products  62.6 us (12%)
  starting transfers between devices  30.8 us (6%)
  local copies, waits for them, and re-layouts  20.8 us (4%)
  between operations  17.3 us (3%)
  other arithmetic  6.25 us (1%)
    all_to_all x1, waiting for transfers between devices, per_device(): lax.all_to_all(jnp.stack([direction_low] * lax.axis_size(RCV)), RCV, 0, 0)  141 us
    psum x10, blocking collectives, one_axis_at_a_time(): value = lax.psum(value, axis)  83.6 us
    all_gather x1, waiting for transfers between devices, per_device(): lax.all_gather(focusing_low, RCV, axis=1, tiled=True)  47.2 us
    dot_general x12, matrix products, contract_time(): return jnp.einsum('tf,frk->trk', table, values, precision=highest)  33.8 us
    all_gather x1, waiting for transfers between devices, all_blocks(): pieces = lax.all_gather(pieces, axes[k])  32.7 us
    all_to_all x3, waiting for transfers between devices, sent_to_all(): lax.all_to_all(jnp.broadcast_to(value[None], (count, *value.shape)), axis...  27.4 us
    dot_general x12, matrix products, contract_back(): return jnp.einsum('tf,trk->frk', table, values, precision=highest)  23.2 us
    all_gather x2, blocking collectives, all_blocks(): pieces = lax.all_gather(pieces, axes[k])  20.7 us
  transfers between devices with their start and end apart: 6, of which 6 were waited for; matrix products, arithmetic and copies ran while one was open for 12% of the time, Pallas kernels for 0%

profile of v1, /device:TPU:4, one launch (start us, length us, event | category | flops | bytes accessed | tf_op | source)
XLA Modules:
  0.0 510.1 jit_solution(17805140955066823009)
XLA Ops:
  8.3 3.0 stack.32
  11.3 13.1 %all-to-all-start = ((bf16[64,2,40,2,192]{4,2,3,1,0:T(8,128)(2,1)}), bf16[64,2,40,2,192]{4,2,3,1,0:T(8,128)(2,1)}, u32[]{:S(2)}, u32[]{:S(2)}) async-start(bf16[64,2,40,2,192]{4,2,3,1,0:T(8,128)(2,1)} %stack.32), calls=%async_computation | async-start | bytes 10485760 | tf_op jit(solution)/shard_map/all_to_all | solution.py:119
  25.1 141.0 %all-to-all-done = bf16[64,2,40,2,192]{4,2,3,1,0:T(8,128)(2,1)} async-done(((bf16[64,2,40,2,192]{4,2,3,1,0:T(8,128)(2,1)}), bf16[64,2,40,2,192]{4,2,3,1,0:T(8,128)(2,1)}, u32[]{:S(2)}, u32[]{:S(2)}) %all-to-all-start) | async-done | bytes 3932192 | tf_op jit(solution)/shard_map/all_to_all | solution.py:119
  166.1 2.8 copy.167
  171.2 5.0 all-to-all-start.1
  177.2 12.5 %all-to-all-done.1 = f32[4,2,40,2,192]{4,1,2,3,0:T(2,128)S(1)} async-done(((f32[4,2,40,2,192]{4,1,2,3,0:T(2,128)}), f32[4,2,40,2,192]{4,1,2,3,0:T(2,128)S(1)}, u32[]{:S(2)}, u32[]{:S(2)}) %all-to-all-start.1) | async-done | bytes 491552 | tf_op jit(solution)/shard_map/all_to_all | solution.py:27
  190.4 2.4 fusion.6
  192.8 2.5 add_select_fusion.1
  195.3 1.4 fusion.114
  198.1 2.4 fusion.7
  200.5 2.5 subtract_select_fusion.1
  203.0 1.8 fusion.102
  206.9 7.1 %all-reduce.4 = (f32[]{:T(128)}, f32[]{:T(128)}) all-reduce(f32[]{:T(128)} %multiply_reduce_fusion.2, f32[]{:T(128)} %multiply_reduce_fusion.1), channel_id=1, replica_groups=mesh['freq_0'=2,'freq_1'=2,'rcv_0'=4,'rcv_1'=8,'rcv_2'=2] {'freq_0'}, use_global_device_ids=true, to_apply=%region_1.0 | all-reduce | flops 2 | bytes 16 | tf_op jit(solution)/shard_map/psum | solution.py:38
  213.9 3.1 all-reduce.3
  217.0 10.1 %all-reduce.1 = (f32[]{:T(128)}, f32[]{:T(128)}) all-reduce(f32[]{:T(128)} %get-tuple-element.38, f32[]{:T(128)} %get-tuple-element.39), channel_id=1, replica_groups=mesh['freq_0'=2,'freq_1'=2,'rcv_0'=4,'rcv_1'=8,'rcv_2'=2] {'rcv_0'}, use_global_device_ids=true, to_apply=%region_3.0 | all-reduce | flops 2 | bytes 16 | tf_op jit(solution)/shard_map/psum | solution.py:38
  227.1 14.8 %all-reduce = (f32[]{:T(128)}, f32[]{:T(128)}) all-reduce(f32[]{:T(128)} %get-tuple-element.34, f32[]{:T(128)} %get-tuple-element.35), channel_id=1, replica_groups=mesh['freq_0'=2,'freq_1'=2,'rcv_0'=4,'rcv_1'=8,'rcv_2'=2] {'rcv_1'}, use_global_device_ids=true, to_apply=%region_4.0 | all-reduce | flops 2 | bytes 16 | tf_op jit(solution)/shard_map/psum | solution.py:38
  241.9 5.5 %all-reduce.2 = (f32[]{:T(128)}, f32[]{:T(128)}) all-reduce(f32[]{:T(128)} %get-tuple-element.32, f32[]{:T(128)} %get-tuple-element.33), channel_id=1, replica_groups=mesh['freq_0'=2,'freq_1'=2,'rcv_0'=4,'rcv_1'=8,'rcv_2'=2] {'rcv_2'}, use_global_device_ids=true, to_apply=%region_5.0 | all-reduce | flops 2 | bytes 16 | tf_op jit(solution)/shard_map/psum | solution.py:38
  249.7 19.6 %all_to_all.25 = f32[4,2,40,2,192]{4,1,2,3,0:T(2,128)S(1)} all-to-all(f32[4,2,40,2,192]{4,1,2,3,0:T(2,128)S(1)} %broadcast_in_dim.9), channel_id=1, replica_groups=mesh['freq_0'=2,'freq_1'=2,'rcv_0'=4,'rcv_1'=8,'rcv_2'=2] {'freq_0','fre..., dimensions={0} | all-to-all | bytes 983040 | tf_op jit(solution)/shard_map/all_to_all | solution.py:27
  270.0 2.4 fusion.9
  272.4 2.5 subtract_select_fusion
  274.9 1.4 fusion.98
  276.3 2.4 fusion.8
  278.7 2.5 add_select_fusion
  282.6 1.6 fusion.100
  285.6 6.0 %all_gather.19 = bf16[2,2,40,2,192]{4,2,3,1,0:T(8,128)(2,1)S(1)} all-gather(bf16[1,2,40,2,192]{4,2,3,1,0:T(8,128)(2,1)S(1)} %copy.186), channel_id=1, replica_groups=mesh['freq_0'=2,'freq_1'=2,'rcv_0'=4,'rcv_1'=8,'rcv_2'=2] {'rcv_2'}, dimensions={0}, use_global_device_ids=true | all-gather | bytes 184320 | tf_op jit(solution)/shard_map/all_gather | solution.py:45
  291.6 14.8 %all-gather = bf16[8,2,40,2,192]{4,2,3,1,0:T(8,128)(2,1)} all-gather(bf16[2,2,40,2,192]{4,2,3,1,0:T(8,128)(2,1)S(1)} %all_gather.19), channel_id=2, replica_groups=mesh['freq_0'=2,'freq_1'=2,'rcv_0'=4,'rcv_1'=8,'rcv_2'=2] {'rcv_0'}, dimensions={0}, use_global_device_ids=true | all-gather | bytes 614400 | tf_op jit(solution)/shard_map/all_gather | solution.py:45
  306.4 47.2 %all-gather.5.cloned.1.call-done = bf16[2,2560,2,192]{3,1,2,0:T(8,128)(2,1)} async-done(((bf16[2,40,2,192]{3,1,2,0:T(8,128)(2,1)}), bf16[2,2560,2,192]{3,1,2,0:T(8,128)(2,1)}) %all-gather.5.cloned.1.call-update) | async-done | bytes 3932176 | tf_op jit(solution)/shard_map/all_gather | solution.py:136
  353.6 3.5 fusion
  358.3 5.0 all-to-all-start.3
  364.0 7.9 %all-to-all-done.3 = f32[4,2,40,2,192]{4,1,2,3,0:T(2,128)S(1)} async-done(((f32[4,2,40,2,192]{4,1,2,3,0:T(2,128)}), f32[4,2,40,2,192]{4,1,2,3,0:T(2,128)S(1)}, u32[]{:S(2)}, u32[]{:S(2)}) %all-to-all-start.3) | async-done | bytes 491552 | tf_op jit(solution)/shard_map/all_to_all | solution.py:27
  372.6 2.4 fusion.10
  375.0 3.9 fusion.11
  378.8 3.7 add_multiply_fusion
  382.6 32.7 %all-gather.7.cloned.1.call-done = bf16[32,2,2,40,2,192]{5,3,4,2,1,0:T(8,128)(2,1)} async-done(((bf16[4,2,2,40,2,192]{5,3,4,2,1,0:T(8,128)(2,1)}), bf16[32,2,2,40,2,192]{5,3,4,2,1,0:T(8,128)(2,1)}) %all-gather.7.cloned.1.call-update) | async-done | bytes 3932176 | tf_op jit(solution)/shard_map/all_gather | solution.py:45
  415.2 3.0 copy.187
  421.2 4.3 subtract_multiply_fusion
  425.5 7.1 %psum.115 = f32[]{:T(128)} all-reduce(f32[]{:T(128)} %multiply_reduce_fusion), channel_id=1, replica_groups=mesh['freq_0'=2,'freq_1'=2,'rcv_0'=4,'rcv_1'=8,'rcv_2'=2] {'freq_0'}, use_global_device_ids=true, to_apply=%region_13.0 | all-reduce | flops 1 | bytes 8 | tf_op jit(solution)/shard_map/psum | solution.py:38
  432.6 3.8 fusion.108
  436.3 3.3 psum.116
  439.6 3.7 fusion.94
  443.4 11.1 %psum.117 = f32[]{:T(128)} all-reduce(f32[]{:T(128)} %psum.116), channel_id=1, replica_groups=mesh['freq_0'=2,'freq_1'=2,'rcv_0'=4,'rcv_1'=8,'rcv_2'=2] {'rcv_0'}, use_global_device_ids=true, to_apply=%region_15.0 | all-reduce | flops 1 | bytes 8 | tf_op jit(solution)/shard_map/psum | solution.py:38
  454.4 2.0 fusion.96
  456.5 16.1 %psum.118 = f32[]{:T(128)} all-reduce(f32[]{:T(128)} %psum.117), channel_id=1, replica_groups=mesh['freq_0'=2,'freq_1'=2,'rcv_0'=4,'rcv_1'=8,'rcv_2'=2] {'rcv_1'}, use_global_device_ids=true, to_apply=%region_16.0 | all-reduce | flops 1 | bytes 8 | tf_op jit(solution)/shard_map/psum | solution.py:38
  472.6 2.0 fusion.106
  474.6 5.5 %psum.119 = f32[]{:T(128)} all-reduce(f32[]{:T(128)} %psum.118), channel_id=1, replica_groups=mesh['freq_0'=2,'freq_1'=2,'rcv_0'=4,'rcv_1'=8,'rcv_2'=2] {'rcv_2'}, use_global_device_ids=true, to_apply=%region_17.0 | all-reduce | flops 1 | bytes 8 | tf_op jit(solution)/shard_map/psum | solution.py:38
  483.8 7.5 %all-to-all-start.4 = ((f32[64,2,2,192]{3,2,1,0:T(2,128)}), f32[64,2,2,192]{3,2,1,0:T(2,128)S(1)}, u32[]{:S(2)}, u32[]{:S(2)}) async-start(f32[64,2,2,192]{3,2,1,0:T(2,128)} %broadcast_in_dim.11), calls=%async_computation.4 | async-start | bytes 524288 | tf_op jit(solution)/shard_map/all_to_all | solution.py:27
  491.3 1.7 copy.205
  495.4 6.9 %all-to-all-done.4 = f32[64,2,2,192]{3,2,1,0:T(2,128)S(1)} async-done(((f32[64,2,2,192]{3,2,1,0:T(2,128)}), f32[64,2,2,192]{3,2,1,0:T(2,128)S(1)}, u32[]{:S(2)}, u32[]{:S(2)}) %all-to-all-start.4) | async-done | bytes 196640 | tf_op jit(solution)/shard_map/all_to_all | solution.py:27
  (78 shorter events, 24.4 us)
Async XLA Ops:
  7.2 161.8 %copy-start = (bf16[2,2,40,2560]{3,2,1,0:T(8,128)(2,1)S(1)}, bf16[2,2,40,2560]{3,2,1,0:T(8,128)(2,1)}, u32[]{:S(2)}) copy-start(bf16[2,2,40,2560]{3,2,1,0:T(8,128)(2,1)} %param.6) | copy-start | bytes 2457604
  11.3 13.2 %copy-start.8 = (f32[2,40,2,192]{3,2,1,0:T(2,128)S(1)}, f32[2,40,2,192]{3,2,1,0:T(2,128)}, u32[]{:S(2)}) copy-start(f32[2,40,2,192]{3,2,1,0:T(2,128)} %param.8) | copy-start | bytes 368644
  11.3 154.9 %all-to-all-start = ((bf16[64,2,40,2,192]{4,2,3,1,0:T(8,128)(2,1)}), bf16[64,2,40,2,192]{4,2,3,1,0:T(8,128)(2,1)}, u32[]{:S(2)}, u32[]{:S(2)}) async-start(bf16[64,2,40,2,192]{4,2,3,1,0:T(8,128)(2,1)} %stack.32), calls=%async_computation | async-start | bytes 10485760 | tf_op jit(solution)/shard_map/all_to_all | solution.py:119
  24.4 329.2 %all-gather.5.cloned.1.call-start = ((), (), s32[]{:S(2)}) async-start(), calls=%async_computation.5 | async-start | bytes 5324800 | tf_op jit(solution)/shard_map/all_gather | solution.py:136
  170.0 6.4 %copy-start.9 = (f32[2,40,2,192]{3,2,1,0:T(2,128)S(1)}, f32[2,40,2,192]{3,2,1,0:T(2,128)}, u32[]{:S(2)}) copy-start(f32[2,40,2,192]{3,2,1,0:T(2,128)} %param.11) | copy-start | bytes 368644
  171.2 18.5 %all-to-all-start.1 = ((f32[4,2,40,2,192]{4,1,2,3,0:T(2,128)}), f32[4,2,40,2,192]{4,1,2,3,0:T(2,128)S(1)}, u32[]{:S(2)}, u32[]{:S(2)}) async-start(f32[4,2,40,2,192]{4,1,2,3,0:T(2,128)} %broadcast_in_dim.8), calls=%async_computation.1 | async-start | bytes 1310720 | tf_op jit(solution)/shard_map/all_to_all | solution.py:27
  176.2 239.0 %all-gather.7.cloned.1.call-start = ((), (), s32[]{:S(2)}) async-start(), calls=%async_computation.6 | async-start | bytes 5898240 | tf_op jit(solution)/shard_map/all_gather | solution.py:45
  177.2 15.6 %copy-start.4 = (s32[40,192]{1,0:T(8,128)S(1)}, s32[40,192]{1,0:T(8,128)}, u32[]{:S(2)}) copy-start(s32[40,192]{1,0:T(8,128)} %param.7) | copy-start | bytes 92164
  203.0 45.7 %copy-start.10 = (f32[2,40,2,192]{3,2,1,0:T(2,128)S(1)}, f32[2,40,2,192]{3,2,1,0:T(2,128)}, u32[]{:S(2)}) copy-start(f32[2,40,2,192]{3,2,1,0:T(2,128)} %param.9) | copy-start | bytes 368644
  248.8 0.7 copy-start.5
  358.3 13.6 %all-to-all-start.3 = ((f32[4,2,40,2,192]{4,1,2,3,0:T(2,128)}), f32[4,2,40,2,192]{4,1,2,3,0:T(2,128)S(1)}, u32[]{:S(2)}, u32[]{:S(2)}) async-start(f32[4,2,40,2,192]{4,1,2,3,0:T(2,128)} %broadcast_in_dim.10), calls=%async_computation.3 | async-start | bytes 1310720 | tf_op jit(solution)/shard_map/all_to_all | solution.py:27
  372.6 2.4 copy-start.2
  418.3 3.0 copy-start.1
  418.3 3.0 copy-start.3
  419.3 0.6 copy-start.6
  420.0 0.6 copy-start.7
  483.8 18.5 %all-to-all-start.4 = ((f32[64,2,2,192]{3,2,1,0:T(2,128)}), f32[64,2,2,192]{3,2,1,0:T(2,128)S(1)}, u32[]{:S(2)}, u32[]{:S(2)}) async-start(f32[64,2,2,192]{3,2,1,0:T(2,128)} %broadcast_in_dim.11), calls=%async_computation.4 | async-start | bytes 524288 | tf_op jit(solution)/shard_map/all_to_all | solution.py:27
Sparse Core Ops, SparseCore 0:
  27.5 326.0 all-gather.4
  355.4 59.7 all-gather.6
